TPU v7x, 256 devices: a whole 4x4x8 slice. The times are simulated.
256 devices in a mesh: mem: 16 (over z, core), ma: 16 (over x, y).
Axes of the slice: x: 4, y: 4, z: 8, core: 2. Of those that a mesh axis runs over, the one named last changes fastest.
Arguments:
- ar_state: float32 [3, 64, 128, 2, 1280], P(None, 'mem', 'ma'), may hold values from -4 to 4
- forcing: float32 [3, 64, 128, 2, 1280], P(None, 'mem', 'ma'), may hold values from -6 to 6
- ar_decay: float32 [3], replicated, may hold values from 0.3 to 0.95
- amplitude: float32 [3, 1280], replicated, may hold values from 0.05 to 0.4
- wavenumber: int32 [128], replicated, may hold values from 0 to 1279, as said below
- tables: bfloat16 [128, 1280, 1280], P('ma', None, 'mem'), may hold values from -0.15625 to 0.15625
- tendencies: bfloat16 [64, 1280, 5120], P('mem', 'ma'), may hold values from -6 to 6
Outputs:
- perturbed: bfloat16 [64, 1280, 5120], P('mem', 'ma')
- new_state: float32 [3, 64, 128, 2, 1280], P(None, 'mem', 'ma')
Inputs may be any that keep to these rules, and one draw needn't show every extreme that they name: `wavenumber`: 128 distinct values.
All inputs are finite; a program needn't handle non-finite values.
Results may differ from a plain program's by a relative error of at most 0.0042.
Values may be sent and summed in bfloat16 or wider, within the bound.
No kernel may reach another device: no remote copies, remote signals or barrier semaphores. Data moves between devices by JAX's collectives and lax.ppermute only.
A program may use at most 64 MiB of HBM per device.

v0:
```python
import math
import jax
import jax.numpy as jnp
from jax import lax
from jax.sharding import PartitionSpec as P

clip_level = 0.9


def basis_table(wavenumber, lon_count):
    longitude = lax.broadcasted_iota(jnp.int32, (wavenumber.shape[0], lon_count), 1)
    phases = wavenumber[:, None] * longitude % lon_count
    angles = phases.astype(jnp.float32) * (2.0 * math.pi / lon_count)
    stacked = jnp.stack([jnp.cos(angles), -jnp.sin(angles)], axis=1)
    return stacked.reshape(2 * wavenumber.shape[0], lon_count).astype(jnp.bfloat16)


def per_device(ar_state, forcing, ar_decay, amplitude, wavenumber, tables, tendencies):
    local_waves = ar_state.shape[2]
    degree_count = ar_state.shape[4]
    owner_index = lax.axis_index("ma")
    own_waves = lax.dynamic_slice_in_dim(wavenumber, owner_index * local_waves, local_waves)
    degree_grid = lax.broadcasted_iota(jnp.int32, (local_waves, degree_count), 1)
    kept_mask = (degree_grid >= own_waves[:, None]).astype(jnp.float32)
    updated = (
        ar_decay[:, None, None, None, None] * ar_state + amplitude[:, None, None, None, :] * forcing
    )
    new_state = kept_mask[None, None, :, None, :] * updated
    coefficients = jnp.sum(new_state, axis=0).astype(jnp.bfloat16)
    everyone = lax.all_gather(coefficients, "mem", axis=0, tiled=True)
    product = jnp.einsum("bmcn,mnl->blmc", everyone, tables, preferred_element_type=jnp.float32)
    fourier = product.astype(jnp.bfloat16)
    banded = lax.all_to_all(
        lax.all_to_all(fourier, "mem", split_axis=0, concat_axis=1, tiled=True),
        "ma",
        split_axis=1,
        concat_axis=2,
        tiled=True,
    )
    member_count, lat_rows, window_size, reim_parts = banded.shape
    basis = basis_table(wavenumber, tendencies.shape[2])
    fourier_rows = banded.reshape(member_count * lat_rows, window_size * reim_parts)
    pattern = jnp.dot(fourier_rows, basis, preferred_element_type=jnp.float32) * (
        1.0 / math.sqrt(window_size)
    )
    pattern = jnp.clip(pattern, -clip_level, clip_level).reshape(tendencies.shape)
    perturbed = (tendencies.astype(jnp.float32) * (1.0 + pattern)).astype(jnp.bfloat16)
    return (perturbed, new_state)


def solution(mesh):
    return jax.shard_map(
        per_device,
        mesh=mesh,
        in_specs=(
            P(None, "mem", "ma", None, None),
            P(None, "mem", "ma", None, None),
            P(),
            P(),
            P(),
            P("ma", None, "mem"),
            P("mem", "ma", None),
        ),
        out_specs=(P("mem", "ma", None), P(None, "mem", "ma", None, None)),
        check_vma=False,
    )
```

profile of v0, /device:TPU:1, one launch (start us, length us, event | category | flops | bytes accessed | tf_op | source)
XLA Modules:
  0.0 131.1 jit_solution(6090136942241296516)
XLA Ops:
  7.2 0.0 copy-start
  7.2 0.0 all-gather.2.cloned.1.call-start
  7.2 0.8 dynamic_slice.3
  8.1 0.1 fusion.20
  8.1 3.5 %fusion.21 = (bf16[4,8,2,1280]{3,2,1,0:T(2,128)(2,1)S(1)}, f32[3,4,8,2,1280]{4,3,2,1,0:T(2,128)}) fusion(f32[3,4,8,2,1280]{4,3,2,1,0:T(2,128)} %param.8, f32[3,1280]{1,0:T(4,128)} %param.10, f32[3,4,8,2,1280]{4,3,2,1,0:T(2,128)} %param.7, f32[3]{0:T(128)} %param.9, f32[8,1280]{1,0:T(8,128)S(1)} %fusion.20), kind=kLoop, calls=%fused_computation.23 | loop fusion | flops 1146880 | bytes 3169292 | tf_op jit(solution)/shard_map/reduce_sum | solution.py:29
  11.6 0.7 copy.23
  12.3 0.0 all-gather.2.cloned.1.call-update
  12.3 0.0 copy-start.2
  12.3 44.4 %all-gather.2.cloned.1.call-done = bf16[64,8,2,1280]{3,1,2,0:T(8,128)(2,1)} async-done(((bf16[4,8,2,1280]{3,1,2,0:T(8,128)(2,1)}), bf16[64,8,2,1280]{3,1,2,0:T(8,128)(2,1)}) %all-gather.2.cloned.1.call-update) | async-done | bytes 2621456 | tf_op jit(solution)/shard_map/all_gather | solution.py:30
  56.7 0.0 copy-done
  56.7 2.7 %fusion.15 = bf16[64,80,8,2]{1,0,3,2:T(8,128)(2,1)S(1)} fusion(bf16[8,1280,80]{1,2,0:T(8,128)(2,1)S(1)} %copy-done, bf16[64,8,2,1280]{3,1,2,0:T(8,128)(2,1)} %all-gather.2.cloned.1.call-done), kind=kOutput, calls=%fused_computation.18 | convolution fusion | flops 209797120 | bytes 4423680 | tf_op jit(solution)/shard_map/bmcn,mnl->blmc/dot_general | solution.py:31
  59.4 1.0 copy.25
  60.4 4.6 %all-to-all-start = ((bf16[64,80,8,2]{1,3,2,0:T(2,128)(2,1)}), bf16[64,80,8,2]{1,3,2,0:T(2,128)(2,1)S(1)}, u32[]{:S(2)}, u32[]{:S(2)}) async-start(bf16[64,80,8,2]{1,3,2,0:T(2,128)(2,1)} %copy.25), calls=%async_computation | async-start | bytes 524288 | tf_op jit(solution)/shard_map/all_to_all | solution.py:34
  65.0 0.0 copy-done.2
  65.0 12.1 %cosine_convert_fusion = (bf16[128,1,5120]{2,0,1:T(8,128)(2,1)S(1)}, bf16[128,1,5120]{2,0,1:T(8,128)(2,1)}) fusion(s32[128]{0:T(128)S(1)} %copy-done.2), kind=kLoop, calls=%fused_computation.11 | loop fusion | flops 7864320 | bytes 2621952 | tf_op jit(solution)/shard_map/convert
  77.1 0.0 all-to-all-done
  77.1 0.2 copy.39
  77.3 4.0 %copy.31 = bf16[4,16,80,8,2]{3,4,0,2,1:T(2,128)(2,1)} copy(bf16[4,16,80,8,2]{2,1,3,4,0:T(8,128)(2,1)S(1)} %bitcast.30) | data formatting | bytes 327680 | tf_op jit(solution)/shard_map/all_to_all | solution.py:34
  81.2 8.6 %reshape.114 = bf16[16,2,2560]{2,1,0:T(2,128)(2,1)} reshape(bf16[1280,4,2,8]{3,2,1,0:T(2,128)(2,1)} %bitcast.26) | data formatting | bytes 327680
  89.8 6.5 %all-to-all-start.1 = ((bf16[16,2,2560]{2,1,0:T(2,128)(2,1)}), bf16[16,2,2560]{2,1,0:T(2,128)(2,1)S(1)}, u32[]{:S(2)}, u32[]{:S(2)}) async-start(bf16[16,2,2560]{2,1,0:T(2,128)(2,1)} %reshape.114), calls=%async_computation.1 | async-start | bytes 327680 | tf_op jit(solution)/shard_map/all_to_all | solution.py:33
  96.4 1.6 %pad_maximum_fusion = bf16[128,2,5120]{2,0,1:T(8,128)(2,1)S(1)} fusion(bf16[128,1,5120]{2,0,1:T(8,128)(2,1)} %get-tuple-element.5, bf16[128,1,5120]{2,0,1:T(8,128)(2,1)S(1)} %get-tuple-element.4), kind=kLoop, calls=%fused_computation.7 | loop fusion | flops 1310720 | bytes 5242880 | tf_op jit(solution)/shard_map/stack | solution.py:14
  97.9 4.2 %copy.29 = bf16[128,2,5120]{2,1,0:T(2,128)(2,1)} copy(bf16[128,2,5120]{2,0,1:T(8,128)(2,1)S(1)} %pad_maximum_fusion) | data formatting | bytes 5242880 | tf_op jit(solution)/shard_map/stack | solution.py:14
  102.1 6.5 %convert_element_type.52 = bf16[256,5120]{1,0:T(8,128)(2,1)} reshape(bf16[128,2,5120]{2,1,0:T(2,128)(2,1)} %copy.29) | data formatting | bytes 5242880 | tf_op jit(solution)/shard_map/convert_element_type | solution.py:15
  108.6 0.0 all-to-all-done.1
  108.6 4.1 %reshape.115 = bf16[1280,4,2,8]{3,2,1,0:T(2,128)(2,1)} reshape(bf16[16,2,2560]{2,1,0:T(2,128)(2,1)S(1)} %all-to-all-done.1) | data formatting | bytes 327680
  112.7 5.2 %copy.28 = bf16[4,16,80,8,2]{2,0,4,3,1:T(4,128)(2,1)S(1)} copy(bf16[4,16,80,8,2]{3,4,0,2,1:T(2,128)(2,1)} %bitcast.27) | data formatting | bytes 327680 | tf_op jit(solution)/shard_map/all_to_all | solution.py:33
  117.9 0.2 reshape.112
  118.1 0.0 copy-start.1
  118.1 3.4 %fusion.1 = f32[320,5120]{1,0:T(8,128)S(1)} fusion(bf16[320,256]{0,1:T(8,128)(2,1)S(1)} %reshape.112, bf16[256,5120]{1,0:T(8,128)(2,1)} %convert_element_type.52), kind=kOutput, calls=%fused_computation.2 | convolution fusion | flops 843776000 | bytes 9338880 | tf_op jit(solution)/shard_map/dot_general | solution.py:43
  121.6 0.0 copy-done.1
  121.6 2.7 %multiply_convert_fusion = bf16[4,80,5120]{2,1,0:T(8,128)(2,1)} fusion(f32[4,80,5120]{2,1,0:T(8,128)S(1)} %bitcast.25, bf16[4,80,5120]{2,1,0:T(8,128)(2,1)S(1)} %copy-done.1), kind=kLoop, calls=%fused_computation.3 | loop fusion | flops 4915200 | bytes 13107200 | tf_op jit(solution)/shard_map/convert_element_type | solution.py:47
Async XLA Ops:
  7.2 49.6 %copy-start = (bf16[8,1280,80]{1,2,0:T(8,128)(2,1)S(1)}, bf16[8,1280,80]{1,2,0:T(8,128)(2,1)}, u32[]{:S(2)}) copy-start(bf16[8,1280,80]{1,2,0:T(8,128)(2,1)} %param.12) | copy-start | bytes 4915204
  7.2 49.6 %all-gather.2.cloned.1.call-start = ((), (), s32[]{:S(2)}) async-start(), calls=%async_computation.2 | async-start | bytes 2785280 | tf_op jit(solution)/shard_map/all_gather | solution.py:30
  12.3 52.7 %copy-start.2 = (s32[128]{0:T(128)S(1)}, s32[128]{0:T(128)}, u32[]{:S(2)}) copy-start(s32[128]{0:T(128)} %param.11) | copy-start | bytes 1540
  60.4 16.7 %all-to-all-start = ((bf16[64,80,8,2]{1,3,2,0:T(2,128)(2,1)}), bf16[64,80,8,2]{1,3,2,0:T(2,128)(2,1)S(1)}, u32[]{:S(2)}, u32[]{:S(2)}) async-start(bf16[64,80,8,2]{1,3,2,0:T(2,128)(2,1)} %copy.25), calls=%async_computation | async-start | bytes 524288 | tf_op jit(solution)/shard_map/all_to_all | solution.py:34
  89.8 18.8 %all-to-all-start.1 = ((bf16[16,2,2560]{2,1,0:T(2,128)(2,1)}), bf16[16,2,2560]{2,1,0:T(2,128)(2,1)S(1)}, u32[]{:S(2)}, u32[]{:S(2)}) async-start(bf16[16,2,2560]{2,1,0:T(2,128)(2,1)} %reshape.114), calls=%async_computation.1 | async-start | bytes 327680 | tf_op jit(solution)/shard_map/all_to_all | solution.py:33
  118.1 3.4 %copy-start.1 = (bf16[4,80,5120]{2,1,0:T(8,128)(2,1)S(1)}, bf16[4,80,5120]{2,1,0:T(8,128)(2,1)}, u32[]{:S(2)}) copy-start(bf16[4,80,5120]{2,1,0:T(8,128)(2,1)} %param.13) | copy-start | bytes 9830404
Sparse Core Ops, SparseCore 0:
  12.4 44.2 all-gather.1
where the time goes:
time: 132 us; the launch traced here: 131 us
  waiting for transfers between devices  44.4 us (34%)
  local copies, waits for them, and re-layouts  35.5 us (27%)
  other arithmetic  19.9 us (15%)
  between operations  14.1 us (11%)
  starting transfers between devices  11.2 us (8%)
  matrix products  6.1 us (5%)
    all_gather x1, waiting for transfers between devices, per_device(): everyone = lax.all_gather(coefficients, 'mem', axis=0, tiled=True)  44.4 us
    unnamed x8, local copies, waits for them, and re-layouts  12.8 us
    another operation x1, other arithmetic  12.1 us
    all_to_all x1, starting transfers between devices, per_device(): lax.all_to_all(lax.all_to_all(fourier, 'mem', split_axis=0, concat_axis=1...  6.53 us
    convert_element_type x1, local copies, waits for them, and re-layouts, basis_table(): stacked.reshape(2 * wavenumber.shape[0], lon_count).astype(jnp.bfloat16)  6.47 us
    all_to_all x1, local copies, waits for them, and re-layouts, per_device(): lax.all_to_all(lax.all_to_all(fourier, 'mem', split_axis=0, concat_axis=1...  5.18 us
    all_to_all x1, starting transfers between devices, per_device(): lax.all_to_all(fourier, 'mem', split_axis=0, concat_axis=1, tiled=True)  4.59 us
    another operation x1, local copies, waits for them, and re-layouts, basis_table(): stacked = jnp.stack([jnp.cos(angles), -jnp.sin(angles)], axis=1)  4.19 us
  transfers between devices with their start and end apart: 3, of which 1 were waited for; matrix products, arithmetic and copies ran while one was open for 19% of the time, Pallas kernels for 0%

commit v1 on v0

--- a/solution.py
+++ b/solution.py
@@ -5,6 +5,28 @@
 from jax.sharding import PartitionSpec as P
 
 clip_level = 0.9
+
+
+def laid_out(tiles, dim):
+    shape = list(tiles.shape[1:])
+    shape[dim] *= tiles.shape[0]
+    return jnp.moveaxis(tiles, 0, dim).reshape(shape)
+
+
+def ring_gather(x, axis, dim):
+    size = lax.axis_size(axis)
+    pairs = [(i, (i + 1) % size) for i in range(size)]
+    back = [(b, a) for a, b in pairs]
+    lower, upper = ([], [])
+    for step in range(size - 1):
+        if step % 2 == 0:
+            lower.append(lax.ppermute(lower[-1] if lower else x, axis, pairs))
+        else:
+            upper.append(lax.ppermute(upper[-1] if upper else x, axis, back))
+    blocks = jnp.stack([*lower[::-1], x, *upper])
+    shift = lax.axis_index(axis) - len(lower)
+    blocks = blocks[(jnp.arange(size) - shift) % size]
+    return laid_out(blocks, dim)
 
 
 def basis_table(wavenumber, lon_count):
@@ -27,7 +49,7 @@
     )
     new_state = kept_mask[None, None, :, None, :] * updated
     coefficients = jnp.sum(new_state, axis=0).astype(jnp.bfloat16)
-    everyone = lax.all_gather(coefficients, "mem", axis=0, tiled=True)
+    everyone = ring_gather(coefficients, "mem", 0)
     product = jnp.einsum("bmcn,mnl->blmc", everyone, tables, preferred_element_type=jnp.float32)
     fourier = product.astype(jnp.bfloat16)
     banded = lax.all_to_all(

time: 132 us -> 144 us (1.091)
  starting transfers between devices: 11.2 us -> 55.6 us
  waiting for transfers between devices: 44.4 us -> 9.39 us
  local copies, waits for them, and re-layouts: 35.5 us -> 51.4 us
  between operations: 14.1 us -> 0.75 us
    all_gather x1 -> x0, waiting for transfers between devices: 44.4 us -> none  [per_device(): everyone = lax.all_gather(coefficients, 'mem', axis=0, tiled=True)]
    ppermute x0 -> x15, starting transfers between devices: none -> 37.6 us  [the longest x7 29.7 us: ring_gather(): upper.append(lax.ppermute(upper[-1] if upper else x, axis, back))]
    unnamed x8 -> x23, local copies, waits for them, and re-layouts: 12.8 us -> 24.8 us
    ppermute x0 -> x15, waiting for transfers between devices: none -> 9.38 us  [the longest x8 9.07 us: ring_gather(): lower.append(lax.ppermute(lower[-1] if lower else x, axis, pairs))]
    all_to_all x1, starting transfers between devices: 4.59 us -> 11.2 us  [per_device(): lax.all_to_all(fourier, 'mem', split_axis=0, concat_axis=1, tiled=True)]
    gather x0 -> x1, local copies, waits for them, and re-layouts: none -> 3.95 us  [ring_gather(): blocks = blocks[(jnp.arange(size) - shift) % size]]
  transfers between devices with their start and end apart: 3 -> 17, of which waited for: 1 -> 10; matrix products, arithmetic and copies ran while one was open for 19% -> 25% of each run, Pallas kernels for 0% -> 0%
where the time goes in v1:
time: 144 us; the launch traced here: 143 us
  starting transfers between devices  55.6 us (39%)
  local copies, waits for them, and re-layouts  51.4 us (36%)
  other arithmetic  19.9 us (14%)
  waiting for transfers between devices  9.39 us (7%)
  matrix products  6.11 us (4%)
    ppermute x7, starting transfers between devices, ring_gather(): upper.append(lax.ppermute(upper[-1] if upper else x, axis, back))  29.7 us
    unnamed x23, local copies, waits for them, and re-layouts  24.8 us
    another operation x1, other arithmetic  12.1 us
    all_to_all x1, starting transfers between devices, per_device(): lax.all_to_all(fourier, 'mem', split_axis=0, concat_axis=1, tiled=True)  11.2 us
    ppermute x8, waiting for transfers between devices, ring_gather(): lower.append(lax.ppermute(lower[-1] if lower else x, axis, pairs))  9.07 us
    ppermute x8, starting transfers between devices, ring_gather(): lower.append(lax.ppermute(lower[-1] if lower else x, axis, pairs))  7.95 us
    all_to_all x1, starting transfers between devices, per_device(): lax.all_to_all(lax.all_to_all(fourier, 'mem', split_axis=0, concat_axis=1...  6.76 us
    convert_element_type x1, local copies, waits for them, and re-layouts, basis_table(): stacked.reshape(2 * wavenumber.shape[0], lon_count).astype(jnp.bfloat16)  6.49 us
  transfers between devices with their start and end apart: 17, of which 10 were waited for; matrix products, arithmetic and copies ran while one was open for 25% of the time, Pallas kernels for 0%

profile of v1, /device:TPU:1, one launch (start us, length us, event | category | flops | bytes accessed | tf_op | source)
XLA Modules:
  0.0 143.2 jit_solution(16881253127821123155)
XLA Ops:
  1.6 3.5 %fusion.23 = (bf16[4,8,2,1280]{3,2,1,0:T(2,128)(2,1)S(1)}, f32[3,4,8,2,1280]{4,3,2,1,0:T(2,128)}) fusion(f32[3,4,8,2,1280]{4,3,2,1,0:T(2,128)} %param.8, f32[3,1280]{1,0:T(4,128)} %param.10, f32[3,4,8,2,1280]{4,3,2,1,0:T(2,128)} %param.7, f32[3]{0:T(128)} %param.9, f32[8,1280]{1,0:T(8,128)S(1)} %fusion.20), kind=kLoop, calls=%fused_computation.48 | loop fusion | flops 1146880 | bytes 3169292 | tf_op jit(solution)/shard_map/reduce_sum | solution.py:51
  5.1 3.0 %collective-permute-start = (bf16[4,8,2,1280]{3,1,2,0:T(8,128)(2,1)S(1)}, bf16[4,8,2,1280]{3,1,2,0:T(8,128)(2,1)S(1)}, u32[]{:S(2)}, u32[]{:S(2)}) collective-permute-start(bf16[4,8,2,1280]{3,1,2,0:T(8,128)(2,1)S(1)} %copy.41), channel_id=1, source_target_pairs={{0,16},{16,32},{32,48},{48,64},{64,80},{80,96},{96,112},{112,128},... | collective-permute-start | bytes 491528 | tf_op jit(solution)/shard_map/ppermute | solution.py:23
  8.1 2.3 %collective-permute-done = bf16[4,8,2,1280]{3,1,2,0:T(8,128)(2,1)S(1)} collective-permute-done((bf16[4,8,2,1280]{3,1,2,0:T(8,128)(2,1)S(1)}, bf16[4,8,2,1280]{3,1,2,0:T(8,128)(2,1)S(1)}, u32[]{:S(2)}, u32[]{:S(2)}) %collective-permute-start) | collective-permute-done | bytes 163872 | tf_op jit(solution)/shard_map/ppermute | solution.py:23
  10.4 2.5 %collective-permute-start.1 = (bf16[4,8,2,1280]{3,1,2,0:T(8,128)(2,1)S(1)}, bf16[4,8,2,1280]{3,1,2,0:T(8,128)(2,1)S(1)}, u32[]{:S(2)}, u32[]{:S(2)}) collective-permute-start(bf16[4,8,2,1280]{3,1,2,0:T(8,128)(2,1)S(1)} %collective-permute-done), channel_id=1, source_target_pairs={{0,16},{16,32},{32,48},{48,64},{64,80},{80,96},{96,112},{112,128},... | collective-permute-start | bytes 491528 | tf_op jit(solution)/shard_map/ppermute | solution.py:23
  12.8 2.0 %collective-permute-start.8 = (bf16[4,8,2,1280]{3,1,2,0:T(8,128)(2,1)S(1)}, bf16[4,8,2,1280]{3,1,2,0:T(8,128)(2,1)S(1)}, u32[]{:S(2)}, u32[]{:S(2)}) collective-permute-start(bf16[4,8,2,1280]{3,1,2,0:T(8,128)(2,1)S(1)} %copy.41), channel_id=1, source_target_pairs={{16,0},{32,16},{48,32},{64,48},{80,64},{96,80},{112,96},{128,112},... | collective-permute-start | bytes 491528 | tf_op jit(solution)/shard_map/ppermute | solution.py:25
  15.8 1.8 %collective-permute-start.2 = (bf16[4,8,2,1280]{3,1,2,0:T(8,128)(2,1)S(1)}, bf16[4,8,2,1280]{3,1,2,0:T(8,128)(2,1)S(1)}, u32[]{:S(2)}, u32[]{:S(2)}) collective-permute-start(bf16[4,8,2,1280]{3,1,2,0:T(8,128)(2,1)S(1)} %collective-permute-done.1), channel_id=1, source_target_pairs={{0,16},{16,32},{32,48},{48,64},{64,80},{80,96},{96,112},{112,128},... | collective-permute-start | bytes 491528 | tf_op jit(solution)/shard_map/ppermute | solution.py:23
  17.6 3.2 %collective-permute-start.9 = (bf16[4,8,2,1280]{3,1,2,0:T(8,128)(2,1)S(1)}, bf16[4,8,2,1280]{3,1,2,0:T(8,128)(2,1)S(1)}, u32[]{:S(2)}, u32[]{:S(2)}) collective-permute-start(bf16[4,8,2,1280]{3,1,2,0:T(8,128)(2,1)S(1)} %collective-permute-done.8), channel_id=1, source_target_pairs={{16,0},{32,16},{48,32},{64,48},{80,64},{96,80},{112,96},{128,112},... | collective-permute-start | bytes 491528 | tf_op jit(solution)/shard_map/ppermute | solution.py:25
  22.3 4.5 %collective-permute-start.10 = (bf16[4,8,2,1280]{3,1,2,0:T(8,128)(2,1)S(1)}, bf16[4,8,2,1280]{3,1,2,0:T(8,128)(2,1)S(1)}, u32[]{:S(2)}, u32[]{:S(2)}) collective-permute-start(bf16[4,8,2,1280]{3,1,2,0:T(8,128)(2,1)S(1)} %collective-permute-done.9), channel_id=1, source_target_pairs={{16,0},{32,16},{48,32},{64,48},{80,64},{96,80},{112,96},{128,112},... | collective-permute-start | bytes 491528 | tf_op jit(solution)/shard_map/ppermute | solution.py:25
  27.8 4.9 %collective-permute-start.11 = (bf16[4,8,2,1280]{3,1,2,0:T(8,128)(2,1)S(1)}, bf16[4,8,2,1280]{3,1,2,0:T(8,128)(2,1)S(1)}, u32[]{:S(2)}, u32[]{:S(2)}) collective-permute-start(bf16[4,8,2,1280]{3,1,2,0:T(8,128)(2,1)S(1)} %collective-permute-done.10), channel_id=1, source_target_pairs={{16,0},{32,16},{48,32},{64,48},{80,64},{96,80},{112,96},{128,112},... | collective-permute-start | bytes 491528 | tf_op jit(solution)/shard_map/ppermute | solution.py:25
  33.8 4.9 %collective-permute-start.12 = (bf16[4,8,2,1280]{3,1,2,0:T(8,128)(2,1)S(1)}, bf16[4,8,2,1280]{3,1,2,0:T(8,128)(2,1)S(1)}, u32[]{:S(2)}, u32[]{:S(2)}) collective-permute-start(bf16[4,8,2,1280]{3,1,2,0:T(8,128)(2,1)S(1)} %collective-permute-done.11), channel_id=1, source_target_pairs={{16,0},{32,16},{48,32},{64,48},{80,64},{96,80},{112,96},{128,112},... | collective-permute-start | bytes 491528 | tf_op jit(solution)/shard_map/ppermute | solution.py:25
  38.7 1.0 collective-permute-done.5
  39.7 5.0 %collective-permute-start.13 = (bf16[4,8,2,1280]{3,1,2,0:T(8,128)(2,1)S(1)}, bf16[4,8,2,1280]{3,1,2,0:T(8,128)(2,1)S(1)}, u32[]{:S(2)}, u32[]{:S(2)}) collective-permute-start(bf16[4,8,2,1280]{3,1,2,0:T(8,128)(2,1)S(1)} %collective-permute-done.12), channel_id=1, source_target_pairs={{16,0},{32,16},{48,32},{64,48},{80,64},{96,80},{112,96},{128,112},... | collective-permute-start | bytes 491528 | tf_op jit(solution)/shard_map/ppermute | solution.py:25
  44.8 1.2 collective-permute-done.6
  46.0 5.1 %collective-permute-start.14 = (bf16[4,8,2,1280]{3,1,2,0:T(8,128)(2,1)S(1)}, bf16[4,8,2,1280]{3,1,2,0:T(8,128)(2,1)S(1)}, u32[]{:S(2)}, u32[]{:S(2)}) collective-permute-start(bf16[4,8,2,1280]{3,1,2,0:T(8,128)(2,1)S(1)} %collective-permute-done.13), channel_id=1, source_target_pairs={{16,0},{32,16},{48,32},{64,48},{80,64},{96,80},{112,96},{128,112},... | collective-permute-start | bytes 491528 | tf_op jit(solution)/shard_map/ppermute | solution.py:25
  51.1 1.0 collective-permute-done.7
  52.8 1.6 %bitcast_dynamic-update-slice_fusion.14 = bf16[16,4,8,2,1280]{4,2,3,1,0:T(8,128)(2,1)} fusion(bf16[16,4,8,2,1280]{4,2,3,1,0:T(8,128)(2,1)} %bitcast_dynamic-update-slice_fusion.15, bf16[4,8,2,1280]{3,1,2,0:T(8,128)(2,1)} %collective-permute-done.6), kind=kLoop, calls=%fused_computation.37 | loop fusion | bytes 327680
  54.4 1.6 %bitcast_dynamic-update-slice_fusion.13 = bf16[16,4,8,2,1280]{4,2,3,1,0:T(8,128)(2,1)} fusion(bf16[16,4,8,2,1280]{4,2,3,1,0:T(8,128)(2,1)} %bitcast_dynamic-update-slice_fusion.14, bf16[4,8,2,1280]{3,1,2,0:T(8,128)(2,1)} %collective-permute-done.5), kind=kLoop, calls=%fused_computation.36 | loop fusion | bytes 327680
  64.8 3.9 %gather_fusion = bf16[16,4,8,2,1280]{4,2,3,1,0:T(8,128)(2,1)} fusion(bf16[16,4,8,2,1280]{4,2,3,1,0:T(8,128)(2,1)} %bitcast_dynamic-update-slice_fusion, s32[1024]{0:T(1024)S(1)} %pad_clamp_fusion), kind=kCustom, calls=%fused_computation | custom fusion | bytes 5242944 | tf_op jit(solution)/shard_map/gather | solution.py:28
  68.8 2.7 %fusion.15 = bf16[64,80,8,2]{1,0,3,2:T(8,128)(2,1)S(1)} fusion(bf16[8,1280,80]{1,2,0:T(8,128)(2,1)S(1)} %copy-done, bf16[64,8,2,1280]{3,1,2,0:T(8,128)(2,1)} %bitcast.63), kind=kOutput, calls=%fused_computation.19 | convolution fusion | flops 209797120 | bytes 4423680 | tf_op jit(solution)/shard_map/bmcn,mnl->blmc/dot_general | solution.py:53
  71.5 1.0 copy.26
  72.4 11.2 %all-to-all-start = ((bf16[64,80,8,2]{1,3,2,0:T(2,128)(2,1)}), bf16[64,80,8,2]{1,3,2,0:T(2,128)(2,1)S(1)}, u32[]{:S(2)}, u32[]{:S(2)}) async-start(bf16[64,80,8,2]{1,3,2,0:T(2,128)(2,1)} %copy.26), calls=%async_computation | async-start | bytes 524288 | tf_op jit(solution)/shard_map/all_to_all | solution.py:56
  83.6 12.1 %cosine_convert_fusion = (bf16[128,1,5120]{2,0,1:T(8,128)(2,1)S(1)}, bf16[128,1,5120]{2,0,1:T(8,128)(2,1)}) fusion(s32[128]{0:T(128)S(1)} %copy-done.2), kind=kLoop, calls=%fused_computation.12 | loop fusion | flops 7864320 | bytes 2621952 | tf_op jit(solution)/shard_map/convert
  95.9 4.0 %copy.32 = bf16[4,16,80,8,2]{3,4,0,2,1:T(2,128)(2,1)} copy(bf16[4,16,80,8,2]{2,1,3,4,0:T(8,128)(2,1)S(1)} %bitcast.66) | data formatting | bytes 327680 | tf_op jit(solution)/shard_map/all_to_all | solution.py:56
  99.8 8.6 %reshape.183 = bf16[16,2,2560]{2,1,0:T(2,128)(2,1)} reshape(bf16[1280,4,2,8]{3,2,1,0:T(2,128)(2,1)} %bitcast.61) | data formatting | bytes 327680
  108.5 6.8 %all-to-all-start.1 = ((bf16[16,2,2560]{2,1,0:T(2,128)(2,1)}), bf16[16,2,2560]{2,1,0:T(2,128)(2,1)S(1)}, u32[]{:S(2)}, u32[]{:S(2)}) async-start(bf16[16,2,2560]{2,1,0:T(2,128)(2,1)} %reshape.183), calls=%async_computation.1 | async-start | bytes 327680 | tf_op jit(solution)/shard_map/all_to_all | solution.py:55
  115.2 1.6 %pad_maximum_fusion = bf16[128,2,5120]{2,0,1:T(8,128)(2,1)S(1)} fusion(bf16[128,1,5120]{2,0,1:T(8,128)(2,1)} %get-tuple-element.5, bf16[128,1,5120]{2,0,1:T(8,128)(2,1)S(1)} %get-tuple-element.4), kind=kLoop, calls=%fused_computation.8 | loop fusion | flops 1310720 | bytes 5242880 | tf_op jit(solution)/shard_map/stack | solution.py:36
  116.8 4.2 %copy.30 = bf16[128,2,5120]{2,1,0:T(2,128)(2,1)} copy(bf16[128,2,5120]{2,0,1:T(8,128)(2,1)S(1)} %pad_maximum_fusion) | data formatting | bytes 5242880 | tf_op jit(solution)/shard_map/stack | solution.py:36
  121.0 6.5 %convert_element_type.63 = bf16[256,5120]{1,0:T(8,128)(2,1)} reshape(bf16[128,2,5120]{2,1,0:T(2,128)(2,1)} %copy.30) | data formatting | bytes 5242880 | tf_op jit(solution)/shard_map/convert_element_type | solution.py:37
  127.5 4.1 %reshape.184 = bf16[1280,4,2,8]{3,2,1,0:T(2,128)(2,1)} reshape(bf16[16,2,2560]{2,1,0:T(2,128)(2,1)S(1)} %all-to-all-done.1) | data formatting | bytes 327680
  131.6 5.2 %copy.29 = bf16[4,16,80,8,2]{2,0,4,3,1:T(4,128)(2,1)S(1)} copy(bf16[4,16,80,8,2]{3,4,0,2,1:T(2,128)(2,1)} %bitcast.62) | data formatting | bytes 327680 | tf_op jit(solution)/shard_map/all_to_all | solution.py:55
  137.0 3.4 %fusion.1 = f32[320,5120]{1,0:T(8,128)S(1)} fusion(bf16[320,256]{0,1:T(8,128)(2,1)S(1)} %reshape.173, bf16[256,5120]{1,0:T(8,128)(2,1)} %convert_element_type.63), kind=kOutput, calls=%fused_computation.3 | convolution fusion | flops 843776000 | bytes 9338880 | tf_op jit(solution)/shard_map/dot_general | solution.py:65
  140.4 2.7 %multiply_convert_fusion = bf16[4,80,5120]{2,1,0:T(8,128)(2,1)} fusion(f32[4,80,5120]{2,1,0:T(8,128)S(1)} %bitcast.60, bf16[4,80,5120]{2,1,0:T(8,128)(2,1)S(1)} %copy-done.1), kind=kLoop, calls=%fused_computation.4 | loop fusion | flops 4915200 | bytes 13107200 | tf_op jit(solution)/shard_map/convert_element_type | solution.py:69
  (45 shorter events, 15.3 us)
Async XLA Ops:
  0.6 68.1 %copy-start = (bf16[8,1280,80]{1,2,0:T(8,128)(2,1)S(1)}, bf16[8,1280,80]{1,2,0:T(8,128)(2,1)}, u32[]{:S(2)}) copy-start(bf16[8,1280,80]{1,2,0:T(8,128)(2,1)} %param.12) | copy-start | bytes 4915204
  5.1 5.3 %collective-permute-start = (bf16[4,8,2,1280]{3,1,2,0:T(8,128)(2,1)S(1)}, bf16[4,8,2,1280]{3,1,2,0:T(8,128)(2,1)S(1)}, u32[]{:S(2)}, u32[]{:S(2)}) collective-permute-start(bf16[4,8,2,1280]{3,1,2,0:T(8,128)(2,1)S(1)} %copy.41), channel_id=1, source_target_pairs={{0,16},{16,32},{32,48},{48,64},{64,80},{80,96},{96,112},{112,128},... | collective-permute-start | bytes 491528 | tf_op jit(solution)/shard_map/ppermute | solution.py:23
  10.4 5.4 %collective-permute-start.1 = (bf16[4,8,2,1280]{3,1,2,0:T(8,128)(2,1)S(1)}, bf16[4,8,2,1280]{3,1,2,0:T(8,128)(2,1)S(1)}, u32[]{:S(2)}, u32[]{:S(2)}) collective-permute-start(bf16[4,8,2,1280]{3,1,2,0:T(8,128)(2,1)S(1)} %collective-permute-done), channel_id=1, source_target_pairs={{0,16},{16,32},{32,48},{48,64},{64,80},{80,96},{96,112},{112,128},... | collective-permute-start | bytes 491528 | tf_op jit(solution)/shard_map/ppermute | solution.py:23
  12.8 4.7 %collective-permute-start.8 = (bf16[4,8,2,1280]{3,1,2,0:T(8,128)(2,1)S(1)}, bf16[4,8,2,1280]{3,1,2,0:T(8,128)(2,1)S(1)}, u32[]{:S(2)}, u32[]{:S(2)}) collective-permute-start(bf16[4,8,2,1280]{3,1,2,0:T(8,128)(2,1)S(1)} %copy.41), channel_id=1, source_target_pairs={{16,0},{32,16},{48,32},{64,48},{80,64},{96,80},{112,96},{128,112},... | collective-permute-start | bytes 491528 | tf_op jit(solution)/shard_map/ppermute | solution.py:25
  15.8 6.0 %collective-permute-start.2 = (bf16[4,8,2,1280]{3,1,2,0:T(8,128)(2,1)S(1)}, bf16[4,8,2,1280]{3,1,2,0:T(8,128)(2,1)S(1)}, u32[]{:S(2)}, u32[]{:S(2)}) collective-permute-start(bf16[4,8,2,1280]{3,1,2,0:T(8,128)(2,1)S(1)} %collective-permute-done.1), channel_id=1, source_target_pairs={{0,16},{16,32},{32,48},{48,64},{64,80},{80,96},{96,112},{112,128},... | collective-permute-start | bytes 491528 | tf_op jit(solution)/shard_map/ppermute | solution.py:23
  17.6 4.7 %collective-permute-start.9 = (bf16[4,8,2,1280]{3,1,2,0:T(8,128)(2,1)S(1)}, bf16[4,8,2,1280]{3,1,2,0:T(8,128)(2,1)S(1)}, u32[]{:S(2)}, u32[]{:S(2)}) collective-permute-start(bf16[4,8,2,1280]{3,1,2,0:T(8,128)(2,1)S(1)} %collective-permute-done.8), channel_id=1, source_target_pairs={{16,0},{32,16},{48,32},{64,48},{80,64},{96,80},{112,96},{128,112},... | collective-permute-start | bytes 491528 | tf_op jit(solution)/shard_map/ppermute | solution.py:25
  21.7 6.0 %collective-permute-start.3 = (bf16[4,8,2,1280]{3,1,2,0:T(8,128)(2,1)S(1)}, bf16[4,8,2,1280]{3,1,2,0:T(8,128)(2,1)S(1)}, u32[]{:S(2)}, u32[]{:S(2)}) collective-permute-start(bf16[4,8,2,1280]{3,1,2,0:T(8,128)(2,1)S(1)} %collective-permute-done.2), channel_id=1, source_target_pairs={{0,16},{16,32},{32,48},{48,64},{64,80},{80,96},{96,112},{112,128},... | collective-permute-start | bytes 491528 | tf_op jit(solution)/shard_map/ppermute | solution.py:23
  22.3 5.5 %collective-permute-start.10 = (bf16[4,8,2,1280]{3,1,2,0:T(8,128)(2,1)S(1)}, bf16[4,8,2,1280]{3,1,2,0:T(8,128)(2,1)S(1)}, u32[]{:S(2)}, u32[]{:S(2)}) collective-permute-start(bf16[4,8,2,1280]{3,1,2,0:T(8,128)(2,1)S(1)} %collective-permute-done.9), channel_id=1, source_target_pairs={{16,0},{32,16},{48,32},{64,48},{80,64},{96,80},{112,96},{128,112},... | collective-permute-start | bytes 491528 | tf_op jit(solution)/shard_map/ppermute | solution.py:25
  27.7 6.0 %collective-permute-start.4 = (bf16[4,8,2,1280]{3,1,2,0:T(8,128)(2,1)S(1)}, bf16[4,8,2,1280]{3,1,2,0:T(8,128)(2,1)S(1)}, u32[]{:S(2)}, u32[]{:S(2)}) collective-permute-start(bf16[4,8,2,1280]{3,1,2,0:T(8,128)(2,1)S(1)} %collective-permute-done.3), channel_id=1, source_target_pairs={{0,16},{16,32},{32,48},{48,64},{64,80},{80,96},{96,112},{112,128},... | collective-permute-start | bytes 491528 | tf_op jit(solution)/shard_map/ppermute | solution.py:23
  27.8 6.0 %collective-permute-start.11 = (bf16[4,8,2,1280]{3,1,2,0:T(8,128)(2,1)S(1)}, bf16[4,8,2,1280]{3,1,2,0:T(8,128)(2,1)S(1)}, u32[]{:S(2)}, u32[]{:S(2)}) collective-permute-start(bf16[4,8,2,1280]{3,1,2,0:T(8,128)(2,1)S(1)} %collective-permute-done.10), channel_id=1, source_target_pairs={{16,0},{32,16},{48,32},{64,48},{80,64},{96,80},{112,96},{128,112},... | collective-permute-start | bytes 491528 | tf_op jit(solution)/shard_map/ppermute | solution.py:25
  33.6 6.1 %collective-permute-start.5 = (bf16[4,8,2,1280]{3,1,2,0:T(8,128)(2,1)S(1)}, bf16[4,8,2,1280]{3,1,2,0:T(8,128)(2,1)}, u32[]{:S(2)}, u32[]{:S(2)}) collective-permute-start(bf16[4,8,2,1280]{3,1,2,0:T(8,128)(2,1)S(1)} %collective-permute-done.4), channel_id=1, source_target_pairs={{0,16},{16,32},{32,48},{48,64},{64,80},{80,96},{96,112},{112,128},... | collective-permute-start | bytes 491528 | tf_op jit(solution)/shard_map/ppermute | solution.py:23
  33.8 6.0 %collective-permute-start.12 = (bf16[4,8,2,1280]{3,1,2,0:T(8,128)(2,1)S(1)}, bf16[4,8,2,1280]{3,1,2,0:T(8,128)(2,1)S(1)}, u32[]{:S(2)}, u32[]{:S(2)}) collective-permute-start(bf16[4,8,2,1280]{3,1,2,0:T(8,128)(2,1)S(1)} %collective-permute-done.11), channel_id=1, source_target_pairs={{16,0},{32,16},{48,32},{64,48},{80,64},{96,80},{112,96},{128,112},... | collective-permute-start | bytes 491528 | tf_op jit(solution)/shard_map/ppermute | solution.py:25
  39.7 6.3 %collective-permute-start.6 = (bf16[4,8,2,1280]{3,1,2,0:T(8,128)(2,1)}, bf16[4,8,2,1280]{3,1,2,0:T(8,128)(2,1)}, u32[]{:S(2)}, u32[]{:S(2)}) collective-permute-start(bf16[4,8,2,1280]{3,1,2,0:T(8,128)(2,1)} %collective-permute-done.5), channel_id=1, source_target_pairs={{0,16},{16,32},{32,48},{48,64},{64,80},{80,96},{96,112},{112,128},... | collective-permute-start | bytes 491528 | tf_op jit(solution)/shard_map/ppermute | solution.py:23
  39.7 6.3 %collective-permute-start.13 = (bf16[4,8,2,1280]{3,1,2,0:T(8,128)(2,1)S(1)}, bf16[4,8,2,1280]{3,1,2,0:T(8,128)(2,1)S(1)}, u32[]{:S(2)}, u32[]{:S(2)}) collective-permute-start(bf16[4,8,2,1280]{3,1,2,0:T(8,128)(2,1)S(1)} %collective-permute-done.12), channel_id=1, source_target_pairs={{16,0},{32,16},{48,32},{64,48},{80,64},{96,80},{112,96},{128,112},... | collective-permute-start | bytes 491528 | tf_op jit(solution)/shard_map/ppermute | solution.py:25
  46.0 6.1 %collective-permute-start.7 = (bf16[4,8,2,1280]{3,1,2,0:T(8,128)(2,1)}, bf16[4,8,2,1280]{3,1,2,0:T(8,128)(2,1)S(1)}, u32[]{:S(2)}, u32[]{:S(2)}) collective-permute-start(bf16[4,8,2,1280]{3,1,2,0:T(8,128)(2,1)} %collective-permute-done.6), channel_id=1, source_target_pairs={{0,16},{16,32},{32,48},{48,64},{64,80},{80,96},{96,112},{112,128},... | collective-permute-start | bytes 491528 | tf_op jit(solution)/shard_map/ppermute | solution.py:23
  46.0 18.1 %collective-permute-start.14 = (bf16[4,8,2,1280]{3,1,2,0:T(8,128)(2,1)S(1)}, bf16[4,8,2,1280]{3,1,2,0:T(8,128)(2,1)S(1)}, u32[]{:S(2)}, u32[]{:S(2)}) collective-permute-start(bf16[4,8,2,1280]{3,1,2,0:T(8,128)(2,1)S(1)} %collective-permute-done.13), channel_id=1, source_target_pairs={{16,0},{32,16},{48,32},{64,48},{80,64},{96,80},{112,96},{128,112},... | collective-permute-start | bytes 491528 | tf_op jit(solution)/shard_map/ppermute | solution.py:25
  68.8 14.9 %copy-start.2 = (s32[128]{0:T(128)S(1)}, s32[128]{0:T(128)}, u32[]{:S(2)}) copy-start(s32[128]{0:T(128)} %param.11) | copy-start | bytes 1540
  72.4 23.3 %all-to-all-start = ((bf16[64,80,8,2]{1,3,2,0:T(2,128)(2,1)}), bf16[64,80,8,2]{1,3,2,0:T(2,128)(2,1)S(1)}, u32[]{:S(2)}, u32[]{:S(2)}) async-start(bf16[64,80,8,2]{1,3,2,0:T(2,128)(2,1)} %copy.26), calls=%async_computation | async-start | bytes 524288 | tf_op jit(solution)/shard_map/all_to_all | solution.py:56
  108.5 19.0 %all-to-all-start.1 = ((bf16[16,2,2560]{2,1,0:T(2,128)(2,1)}), bf16[16,2,2560]{2,1,0:T(2,128)(2,1)S(1)}, u32[]{:S(2)}, u32[]{:S(2)}) async-start(bf16[16,2,2560]{2,1,0:T(2,128)(2,1)} %reshape.183), calls=%async_computation.1 | async-start | bytes 327680 | tf_op jit(solution)/shard_map/all_to_all | solution.py:55
  137.0 3.4 %copy-start.1 = (bf16[4,80,5120]{2,1,0:T(8,128)(2,1)S(1)}, bf16[4,80,5120]{2,1,0:T(8,128)(2,1)}, u32[]{:S(2)}) copy-start(bf16[4,80,5120]{2,1,0:T(8,128)(2,1)} %param.13) | copy-start | bytes 9830404
